TPU v7x, 32 devices: a whole 2x2x4 slice. The times are simulated.
32 devices in a mesh: gx: 8 (over z, x), gy: 4 (over y, core).
Axes of the slice: x: 2, y: 2, z: 4, core: 2. Of those that a mesh axis runs over, the one named last changes fastest.
Arguments:
- pooled: bfloat16 [4096, 8, 128], P(('gx', 'gy')), may hold values from -6 to 6
- cotangent: bfloat16 [4096, 28, 128], P(('gx', 'gy')), may hold values from -0.09375 to 0.09375
- bilinear: bfloat16 [7, 128, 128], replicated, may hold values from -0.5 to 0.5
- bag_ids: int32 [4096, 8, 4], P(('gx', 'gy')), may hold values from 0 to 8191, as said below
- bag_lens: int32 [4096, 8], P(('gx', 'gy')), may hold values from 1 to 4
- row_home: int32 [8, 8192], replicated, may hold values from 0 to 8191, as said below
Outputs:
- weight_grad: float32 [7, 128, 128], replicated
- table_grad: float32 [8192, 8, 128], P(('gx', 'gy'))
Inputs may be any that keep to these rules, and one draw needn't show every extreme that they name: Each row row_home[f] is a permutation; row r of field f's table is stored at position row_home[f, r] of table_grad's first dimension. Only the first bag_lens entries of a bag are live. The stored position q = row_home[f, bag_ids[sample, f, k]] of an entry lies in the block of 256 positions of device q // 256 (devices in gx+gy order); among all entries of one device's samples, live or not, at most 256 lie in any one device's block; in every device's entries some block is hit exactly 256 times, and one block is hit exactly 256 times by the entries of every device.
All inputs are finite; a program needn't handle non-finite values.
Results may differ from a plain program's by a relative error of at most 0.0035.
Values may be sent and summed in bfloat16 or wider, within the bound.
No kernel may reach another device: no remote copies, remote signals or barrier semaphores. Data moves between devices by JAX's collectives and lax.ppermute only.
A program may use at most 64 MiB of HBM per device.

v0:
```python
import jax
import jax.numpy as jnp
from jax import lax
from jax.sharding import PartitionSpec as P

FIELDS = 8
BAG = 4
R_DEV = 256


def pair_list(fields):
    return [(i, j) for i in range(fields) for j in range(i + 1, fields)]


def on_device(pooled, cotangent, bilinear, bag_ids, bag_lens, row_home):
    pair_order = pair_list(FIELDS)
    samples = pooled.shape[0]
    width = pooled.shape[2]
    projected = jnp.einsum(
        "bfd,fde->bfe", pooled[:, : FIELDS - 1], bilinear, preferred_element_type=jnp.float32
    )
    upper_terms = []
    for i in range(FIELDS - 1):
        running = jnp.zeros((samples, width), jnp.float32)
        for p, (a, c) in enumerate(pair_order):
            if a == i:
                running = running + cotangent[:, p].astype(jnp.float32) * pooled[:, c].astype(
                    jnp.float32
                )
        upper_terms.append(running)
    upper_bf = jnp.stack(upper_terms, 1).astype(jnp.bfloat16)
    local_weight = jnp.einsum(
        "bfd,bfe->fde", pooled[:, : FIELDS - 1], upper_bf, preferred_element_type=jnp.float32
    )
    weight_grad = lax.psum(local_weight, ("gx", "gy"))
    back_terms = jnp.einsum("bfe,fde->bfd", upper_bf, bilinear, preferred_element_type=jnp.float32)
    field_list = []
    for i in range(FIELDS):
        running = back_terms[:, i] if i < FIELDS - 1 else jnp.zeros((samples, width), jnp.float32)
        for p, (a, c) in enumerate(pair_order):
            if c == i:
                running = running + cotangent[:, p].astype(jnp.float32) * projected[:, a]
        field_list.append(running)
    field_grads = jnp.stack(field_list, 1).astype(jnp.bfloat16)
    size_gx = lax.axis_size("gx")
    size_gy = lax.axis_size("gy")
    owners_all = size_gx * size_gy
    entries = samples * FIELDS * BAG
    capacity = max(1, 2 * entries // owners_all)
    sentinel = R_DEV * FIELDS
    field_index = jnp.arange(FIELDS, dtype=jnp.int32)[None, :, None]
    stored = row_home[field_index, bag_ids]
    live = jnp.arange(BAG, dtype=jnp.int32)[None, None, :] < bag_lens[:, :, None]
    owner = (stored // R_DEV).reshape(-1)
    target = jnp.where(live, stored % R_DEV * FIELDS + field_index, sentinel).reshape(-1)
    values = jnp.where(live[:, :, :, None], field_grads[:, :, None, :], jnp.zeros((), jnp.bfloat16))
    values = values.reshape(entries, width)
    block_rows = 128
    blocks = entries // block_rows
    owner_ids = jnp.arange(owners_all, dtype=jnp.int32)
    owner_table = (owner.reshape(blocks, block_rows, 1) == owner_ids[None, None, :]).astype(
        jnp.bfloat16
    )
    row_pos = jnp.arange(block_rows, dtype=jnp.int32)
    earlier = (row_pos[:, None] > row_pos[None, :]).astype(jnp.bfloat16)
    within_all = jnp.einsum("ij,bjo->bio", earlier, owner_table, preferred_element_type=jnp.float32)
    block_totals = jnp.sum(owner_table.astype(jnp.float32), axis=1)
    block_start = jnp.cumsum(block_totals, axis=0) - block_totals
    ahead = within_all + block_start[:, None, :]
    rank = jnp.sum(ahead * owner_table.astype(jnp.float32), axis=2).reshape(-1).astype(jnp.int32)
    place = owner * capacity + rank
    send_values = (
        jnp.zeros((owners_all * capacity, width), jnp.bfloat16)
        .at[place]
        .set(values, unique_indices=True)
    )
    send_target = (
        jnp.full((owners_all * capacity,), sentinel, jnp.int32)
        .at[place]
        .set(target, unique_indices=True)
    )
    send_values = send_values.reshape(size_gx, size_gy, capacity, width)
    send_target = send_target.reshape(size_gx, size_gy, capacity)
    got_values, got_target = (
        lax.all_to_all(
            lax.all_to_all(send_values, "gy", split_axis=1, concat_axis=1, tiled=True),
            "gx",
            split_axis=0,
            concat_axis=0,
            tiled=True,
        ),
        lax.all_to_all(
            lax.all_to_all(send_target, "gy", split_axis=1, concat_axis=1, tiled=True),
            "gx",
            split_axis=0,
            concat_axis=0,
            tiled=True,
        ),
    )
    summed = jax.ops.segment_sum(
        got_values.reshape(-1, width).astype(jnp.float32),
        got_target.reshape(-1),
        num_segments=sentinel + 1,
    )
    table_grad = summed[:sentinel].reshape(R_DEV, FIELDS, width)
    return (weight_grad, table_grad)


def solution(mesh):
    placed = (
        P(("gx", "gy"), None, None),
        P(("gx", "gy"), None, None),
        P(),
        P(("gx", "gy"), None, None),
        P(("gx", "gy"), None),
        P(),
    )
    return jax.shard_map(
        on_device,
        mesh=mesh,
        in_specs=placed,
        out_specs=(P(), P(("gx", "gy"), None, None)),
        check_vma=False,
    )
```

profile of v0, /device:TPU:0, one launch (start us, length us, event | category | flops | bytes accessed | tf_op | source)
XLA Modules:
  0.0 339.2 jit_solution(13678758075913814048)
XLA Ops:
  7.2 0.8 fusion.102
  8.0 0.3 copy.219
  8.2 0.3 reshape.231
  8.5 25.5 %gather_fusion = s32[4096]{0:T(1024)S(1)} fusion(s32[8,8192]{1,0:T(8,128)S(1)} %copy-done, s32[4096]{0:T(1024)S(1)} %reshape.231), kind=kCustom, calls=%fused_computation | custom fusion | bytes 65536 | tf_op jit(solution)/shard_map/gather | solution.py:52
  34.0 0.2 convert_reduce_fusion
  34.3 0.3 fusion.4
  34.7 0.2 iota_compare_fusion
  34.9 0.3 lt.51
  35.3 0.3 add.296
  35.7 15.5 %scatter_custom_fusion = s32[8192]{0:T(1024)S(1)} fusion(s32[4096]{0:T(1024)S(1)} %bitcast.64, s32[4096]{0:T(1024)S(1)} %fusion.98, s32[]{:T(128)} %constant.25.clone.1), kind=kCustom, calls=%fused_computation.188 | custom fusion | bytes 32772 | tf_op jit(solution)/shard_map/scatter | solution.py:80
  51.3 0.6 copy.221
  51.9 4.3 %all-to-all-start = ((s32[8,4,256]{2,0,1:T(8,128)}), s32[8,4,256]{2,0,1:T(8,128)S(1)}, u32[]{:S(2)}, u32[]{:S(2)}) async-start(s32[8,4,256]{2,0,1:T(8,128)} %copy.221), calls=%async_computation | async-start | bytes 65536 | tf_op jit(solution)/shard_map/all_to_all | solution.py:93
  56.3 0.4 fusion.109
  56.8 0.1 copy.244
  56.9 0.1 copy.242
  57.1 0.1 copy.240
  57.2 0.1 copy.233
  57.4 0.1 copy.237
  57.6 0.1 copy.239
  57.7 0.1 copy.241
  57.8 0.1 copy.243
  57.9 0.1 copy.245
  58.1 0.1 copy.238
  58.2 0.1 copy.236
  58.3 0.1 copy.234
  58.5 0.1 copy.249
  58.6 0.1 copy.250
  58.7 0.1 copy.251
  58.8 0.1 copy.252
  59.0 0.1 copy.247
  59.1 0.1 copy.248
  59.2 0.1 copy.253
  59.3 0.1 copy.254
  59.5 0.1 copy.255
  59.6 0.1 copy.256
  59.7 0.1 copy.257
  59.8 0.1 copy.258
  60.0 0.1 copy.259
  60.1 0.1 copy.260
  60.2 0.1 copy.261
  60.3 0.1 copy.262
  60.5 0.1 copy.263
  60.6 0.1 copy.264
  60.7 0.1 copy.265
  61.5 0.2 convolution_bitcast_fusion
  61.7 0.4 copy-done.3
  62.2 0.3 convolution_bitcast_fusion.1
  62.9 0.2 copy.226
  63.1 0.4 broadcast_in_dim.61
  63.4 13.8 %scatter_custom_fusion.1 = bf16[8192,128]{1,0:T(8,128)(2,1)S(1)} fusion(s32[4096]{0:T(1024)S(1)} %bitcast.65, bf16[4096,128]{1,0:T(8,128)(2,1)S(1)} %bitcast.58, bf16[]{:T(256)} %constant.49.clone.1, pred[4096]{0:T(1024)(128)(4,1)S(1)} %lt.51), kind=kCustom, calls=%fused_computation.14 | custom fusion | flops 524288 | bytes 3150848 | tf_op jit(solution)/shard_map/scatter | solution.py:75
  77.2 1.5 copy.227
  78.7 3.6 %all-to-all-start.2 = ((bf16[8,4,256,128]{3,2,0,1:T(8,128)(2,1)}), bf16[8,4,256,128]{3,2,0,1:T(8,128)(2,1)S(1)}, u32[]{:S(2)}, u32[]{:S(2)}) async-start(bf16[8,4,256,128]{3,2,0,1:T(8,128)(2,1)} %copy.227), calls=%async_computation.2 | async-start | bytes 4194304 | tf_op jit(solution)/shard_map/all_to_all | solution.py:86
  82.3 0.6 copy.222
  82.9 25.0 %all-to-all-done.2 = bf16[8,4,256,128]{3,2,0,1:T(8,128)(2,1)S(1)} async-done(((bf16[8,4,256,128]{3,2,0,1:T(8,128)(2,1)}), bf16[8,4,256,128]{3,2,0,1:T(8,128)(2,1)S(1)}, u32[]{:S(2)}, u32[]{:S(2)}) %all-to-all-start.2) | async-done | bytes 2097184 | tf_op jit(solution)/shard_map/all_to_all | solution.py:86
  107.9 6.3 %all-to-all-start.1 = ((s32[8,4,256]{2,1,0:T(4,128)}), s32[8,4,256]{2,1,0:T(4,128)S(1)}, u32[]{:S(2)}, u32[]{:S(2)}) async-start(s32[8,4,256]{2,1,0:T(4,128)} %copy.222), calls=%async_computation.1 | async-start | bytes 65536 | tf_op jit(solution)/shard_map/all_to_all | solution.py:92
  114.2 1.5 copy.228
  115.7 5.2 %all-to-all-done.1 = s32[8,4,256]{2,1,0:T(4,128)S(1)} async-done(((s32[8,4,256]{2,1,0:T(4,128)}), s32[8,4,256]{2,1,0:T(4,128)S(1)}, u32[]{:S(2)}, u32[]{:S(2)}) %all-to-all-start.1) | async-done | bytes 32800 | tf_op jit(solution)/shard_map/all_to_all | solution.py:92
  120.9 3.6 %all-to-all-start.3 = ((bf16[8,4,256,128]{3,2,1,0:T(8,128)(2,1)}), bf16[8,4,256,128]{3,2,1,0:T(8,128)(2,1)S(1)}, u32[]{:S(2)}, u32[]{:S(2)}) async-start(bf16[8,4,256,128]{3,2,1,0:T(8,128)(2,1)} %copy.228), calls=%async_computation.3 | async-start | bytes 4194304 | tf_op jit(solution)/shard_map/all_to_all | solution.py:85
  124.5 0.2 all-reduce.2.cloned.1.call-start
  124.8 1.0 convolution_bitcast_fusion.2
  125.8 147.7 %all-reduce.2.cloned.1.call-done = f32[7,128,128]{1,2,0:T(8,128)} async-done(((f32[7,128,128]{1,2,0:T(8,128)}), f32[7,128,128]{1,2,0:T(8,128)}) %all-reduce.2.cloned.1.call-update) | async-done | bytes 458768 | tf_op jit(solution)/shard_map/psum | solution.py:35
  273.5 2.0 copy.229
  275.5 55.8 %scatter_custom_fusion.2 = f32[2049,128]{1,0:T(8,128)S(1)} fusion(s32[8192]{0:T(1024)S(1)} %bitcast.63, bf16[8192,128]{1,0:T(8,128)(2,1)S(1)} %bitcast.56, f32[]{:T(128)} %constant.21.clone.1), kind=kCustom, calls=%fused_computation.4 | custom fusion | flops 2097152 | bytes 3146244 | tf_op jit(solution)/shard_map/scatter-add | solution.py:100
  331.3 1.0 slice_bitcast_fusion
  (49 shorter events, 1.7 us)
Async XLA Ops:
  7.2 1.3 copy-start
  8.5 26.1 %copy-start.7 = (s32[128,8]{0,1:T(8,128)S(1)}, s32[128,8]{0,1:T(8,128)}, u32[]{:S(2)}) copy-start(s32[128,8]{0,1:T(8,128)} %param.10) | copy-start | bytes 12292
  34.0 22.2 %copy-start.6 = (bf16[128,28,128]{2,0,1:T(8,128)(2,1)S(1)}, bf16[128,28,128]{2,0,1:T(8,128)(2,1)}, u32[]{:S(2)}) copy-start(bf16[128,28,128]{2,0,1:T(8,128)(2,1)} %param.7) | copy-start | bytes 2752516
  34.3 22.0 %copy-start.1 = (bf16[128,8,128]{2,1,0:T(8,128)(2,1)S(1)}, bf16[128,8,128]{2,1,0:T(8,128)(2,1)}, u32[]{:S(2)}) copy-start(bf16[128,8,128]{2,1,0:T(8,128)(2,1)} %param.6) | copy-start | bytes 786436
  51.9 26.8 %all-to-all-start = ((s32[8,4,256]{2,0,1:T(8,128)}), s32[8,4,256]{2,0,1:T(8,128)S(1)}, u32[]{:S(2)}, u32[]{:S(2)}) async-start(s32[8,4,256]{2,0,1:T(8,128)} %copy.221), calls=%async_computation | async-start | bytes 65536 | tf_op jit(solution)/shard_map/all_to_all | solution.py:93
  57.3 4.2 %copy-start.5 = (bf16[7,128,128]{2,1,0:T(8,128)(2,1)S(1)}, bf16[7,128,128]{2,1,0:T(8,128)(2,1)}, u32[]{:S(2)}) copy-start(bf16[7,128,128]{2,1,0:T(8,128)(2,1)} %param.8) | copy-start | bytes 688132
  61.5 0.7 copy-start.3
  78.7 29.2 %all-to-all-start.2 = ((bf16[8,4,256,128]{3,2,0,1:T(8,128)(2,1)}), bf16[8,4,256,128]{3,2,0,1:T(8,128)(2,1)S(1)}, u32[]{:S(2)}, u32[]{:S(2)}) async-start(bf16[8,4,256,128]{3,2,0,1:T(8,128)(2,1)} %copy.227), calls=%async_computation.2 | async-start | bytes 4194304 | tf_op jit(solution)/shard_map/all_to_all | solution.py:86
  107.9 13.0 %all-to-all-start.1 = ((s32[8,4,256]{2,1,0:T(4,128)}), s32[8,4,256]{2,1,0:T(4,128)S(1)}, u32[]{:S(2)}, u32[]{:S(2)}) async-start(s32[8,4,256]{2,1,0:T(4,128)} %copy.222), calls=%async_computation.1 | async-start | bytes 65536 | tf_op jit(solution)/shard_map/all_to_all | solution.py:92
  115.7 9.1 %copy-start.2 = (bf16[128,8,128]{2,1,0:T(8,128)(2,1)S(1)}, bf16[128,8,128]{2,1,0:T(8,128)(2,1)}, u32[]{:S(2)}) copy-start(bf16[128,8,128]{2,1,0:T(8,128)(2,1)} %param.6) | copy-start | bytes 786436
  115.7 9.1 %copy-start.4 = (bf16[128,7,128]{0,2,1:T(8,128)(2,1)S(1)}, bf16[128,7,128]{0,2,1:T(8,128)(2,1)}, u32[]{:S(2)}) copy-start(bf16[128,7,128]{0,2,1:T(8,128)(2,1)} %copy-done.3) | copy-start | bytes 688132
  120.9 154.6 %all-to-all-start.3 = ((bf16[8,4,256,128]{3,2,1,0:T(8,128)(2,1)}), bf16[8,4,256,128]{3,2,1,0:T(8,128)(2,1)S(1)}, u32[]{:S(2)}, u32[]{:S(2)}) async-start(bf16[8,4,256,128]{3,2,1,0:T(8,128)(2,1)} %copy.228), calls=%async_computation.3 | async-start | bytes 4194304 | tf_op jit(solution)/shard_map/all_to_all | solution.py:85
  124.5 149.0 %all-reduce.2.cloned.1.call-start = ((), (), s32[]{:S(2)}) async-start(), calls=%async_computation.4 | async-start | bytes 917504 | tf_op jit(solution)/shard_map/psum | solution.py:35
Sparse Core Ops, SparseCore 0:
  131.2 142.2 all-reduce.1
where the time goes:
time: 340 us; the launch traced here: 339 us
  waiting for transfers between devices  178 us (52%)
  other arithmetic  71.7 us (21%)
  local copies, waits for them, and re-layouts  55.3 us (16%)
  starting transfers between devices  18 us (5%)
  between operations  14.5 us (4%)
    psum x1, waiting for transfers between devices, on_device(): weight_grad = lax.psum(local_weight, ('gx', 'gy'))  148 us
    scatter-add x1, other arithmetic, on_device(): jax.ops.segment_sum(got_values.reshape(-1, width).astype(jnp.float32), go...  55.8 us
    gather x1, local copies, waits for them, and re-layouts, on_device(): stored = row_home[field_index, bag_ids]  25.5 us
    all_to_all x1, waiting for transfers between devices, on_device(): lax.all_to_all(send_values, 'gy', split_axis=1, concat_axis=1, tiled=True)  25 us
    scatter x1, local copies, waits for them, and re-layouts, on_device(): send_target = jnp.full((owners_all * capacity,), sentinel, jnp.int32).at[...  15.5 us
    scatter x1, other arithmetic, on_device(): send_values = jnp.zeros((owners_all * capacity, width), jnp.bfloat16).at[...  13.8 us
    unnamed x55, local copies, waits for them, and re-layouts  6.81 us
  transfers between devices with their start and end apart: 5, of which 3 were waited for; matrix products, arithmetic and copies ran while one was open for 8% of the time, Pallas kernels for 0%

commit v1 on v0

--- a/solution.py
+++ b/solution.py
@@ -2,6 +2,7 @@
 import jax.numpy as jnp
 from jax import lax
 from jax.sharding import PartitionSpec as P
+from jax.lax import all_gather
 
 FIELDS = 8
 BAG = 4
@@ -32,7 +33,8 @@
     local_weight = jnp.einsum(
         "bfd,bfe->fde", pooled[:, : FIELDS - 1], upper_bf, preferred_element_type=jnp.float32
     )
-    weight_grad = lax.psum(local_weight, ("gx", "gy"))
+    choose_bands_in = lambda local_array, mesh_name: all_gather(local_array, mesh_name).sum(axis=0)
+    weight_grad = choose_bands_in(local_weight, mesh_name=("gx", "gy"))
     back_terms = jnp.einsum("bfe,fde->bfd", upper_bf, bilinear, preferred_element_type=jnp.float32)
     field_list = []
     for i in range(FIELDS):

time: 340 us -> 262 us (0.77)
  waiting for transfers between devices: 178 us -> 94 us
  other arithmetic: 71.7 us -> 77.8 us
    psum x1 -> x0, waiting for transfers between devices: 148 us -> none  [on_device(): weight_grad = lax.psum(local_weight, ('gx', 'gy'))]
    all_to_all x1, waiting for transfers between devices: 0.01 us -> 47.3 us  [on_device(): lax.all_to_all(lax.all_to_all(send_values, 'gy', split_axis=1, concat_axi...]
    all_to_all x1, waiting for transfers between devices: 25 us -> 41.4 us  [on_device(): lax.all_to_all(send_values, 'gy', split_axis=1, concat_axis=1, tiled=True)]
    reduce_sum x0 -> x1, other arithmetic: none -> 6.83 us  [on_device(): all_gather(local_array, mesh_name).sum(axis=0)]
    unnamed x55 -> x166, local copies, waits for them, and re-layouts: 6.81 us -> 5.24 us
  transfers between devices with their start and end apart: 5 -> 5, of which waited for: 3 -> 3; matrix products, arithmetic and copies ran while one was open for 8% -> 46% of each run, Pallas kernels for 0% -> 0%
where the time goes in v1:
time: 262 us
  waiting for transfers between devices  94 us (36%)
  other arithmetic  77.8 us (30%)
  local copies, waits for them, and re-layouts  56.6 us (22%)
  starting transfers between devices  17.2 us (7%)
  between operations  15.3 us (6%)
    scatter-add x1, other arithmetic, on_device(): jax.ops.segment_sum(got_values.reshape(-1, width).astype(jnp.float32), go...  55.8 us
    all_to_all x1, waiting for transfers between devices, on_device(): lax.all_to_all(lax.all_to_all(send_values, 'gy', split_axis=1, concat_axi...  47.3 us
    all_to_all x1, waiting for transfers between devices, on_device(): lax.all_to_all(send_values, 'gy', split_axis=1, concat_axis=1, tiled=True)  41.4 us
    gather x1, local copies, waits for them, and re-layouts, on_device(): stored = row_home[field_index, bag_ids]  25.5 us
    scatter x1, local copies, waits for them, and re-layouts, on_device(): send_target = jnp.full((owners_all * capacity,), sentinel, jnp.int32).at[...  15.5 us
    scatter x1, other arithmetic, on_device(): send_values = jnp.zeros((owners_all * capacity, width), jnp.bfloat16).at[...  13.8 us
    reduce_sum x1, other arithmetic, on_device(): all_gather(local_array, mesh_name).sum(axis=0)  6.83 us
    all_to_all x1, starting transfers between devices, on_device(): lax.all_to_all(lax.all_to_all(send_target, 'gy', split_axis=1, concat_axi...  5.51 us
  transfers between devices with their start and end apart: 5, of which 3 were waited for; matrix products, arithmetic and copies ran while one was open for 46% of the time, Pallas kernels for 0%

profile of v1, /device:TPU:0, one launch (start us, length us, event | category | flops | bytes accessed | tf_op | source)
XLA Modules:
  0.0 261.9 jit_solution(16736044657954954828)
XLA Ops:
  7.2 1.0 fusion.108
  8.2 1.1 fusion.107
  9.3 0.4 fusion.109
  9.7 0.1 copy.251
  9.8 0.1 copy.249
  10.0 0.1 copy.247
  10.1 0.1 copy.245
  10.2 0.1 copy.238
  10.4 0.1 copy.240
  10.5 0.1 copy.242
  10.6 0.1 copy.244
  10.7 0.1 copy.246
  10.9 0.1 copy.248
  11.0 0.1 copy.250
  11.1 0.1 copy.243
  11.2 0.1 copy.241
  11.4 0.1 copy.239
  11.5 0.1 copy.254
  11.6 0.1 copy.255
  11.8 0.1 copy.256
  11.9 0.1 copy.257
  12.0 0.1 copy.252
  12.1 0.1 copy.253
  12.4 0.1 copy.259
  12.5 0.1 copy.260
  12.9 0.1 copy.263
  13.0 0.1 copy.264
  13.3 0.1 copy.266
  13.4 0.1 copy.267
  13.6 0.1 copy.268
  13.8 0.1 copy.270
  13.9 0.1 copy.271
  14.7 0.1 copy-done.12
  14.8 0.7 copy-done.3
  15.5 0.2 convolution_bitcast_fusion.2
  15.8 1.0 copy.221
  16.9 0.3 copy.223
  17.1 0.3 reshape.231
  17.4 25.5 %gather_fusion = s32[4096]{0:T(1024)S(1)} fusion(s32[8,8192]{1,0:T(8,128)S(1)} %copy-done, s32[4096]{0:T(1024)S(1)} %reshape.231), kind=kCustom, calls=%fused_computation | custom fusion | bytes 65536 | tf_op jit(solution)/shard_map/gather | solution.py:54
  43.0 0.2 convert_reduce_fusion
  43.3 0.3 fusion.4
  43.7 0.2 iota_compare_fusion
  43.9 0.3 lt.51
  44.4 0.3 add.294
  44.9 15.5 %scatter_custom_fusion = s32[8192]{0:T(1024)S(1)} fusion(s32[4096]{0:T(1024)S(1)} %bitcast.66, s32[4096]{0:T(1024)S(1)} %fusion.98, s32[]{:T(128)} %constant.25.clone.1), kind=kCustom, calls=%fused_computation.188 | custom fusion | bytes 32772 | tf_op jit(solution)/shard_map/scatter | solution.py:82
  60.4 0.6 copy.225
  61.1 4.3 %all-to-all-start = ((s32[8,4,256]{2,0,1:T(8,128)}), s32[8,4,256]{2,0,1:T(8,128)S(1)}, u32[]{:S(2)}, u32[]{:S(2)}) async-start(s32[8,4,256]{2,0,1:T(8,128)} %copy.225), calls=%async_computation | async-start | bytes 65536 | tf_op jit(solution)/shard_map/all_to_all | solution.py:95
  65.4 0.2 convolution_bitcast_fusion
  65.6 0.3 convolution_bitcast_fusion.1
  66.6 0.2 copy.230
  66.8 0.4 broadcast_in_dim.61
  67.2 13.8 %scatter_custom_fusion.1 = bf16[8192,128]{1,0:T(8,128)(2,1)S(1)} fusion(s32[4096]{0:T(1024)S(1)} %bitcast.67, bf16[4096,128]{1,0:T(8,128)(2,1)S(1)} %bitcast.60, bf16[]{:T(256)} %constant.49.clone.1, pred[4096]{0:T(1024)(128)(4,1)S(1)} %lt.51), kind=kCustom, calls=%fused_computation.14 | custom fusion | flops 524288 | bytes 3150848 | tf_op jit(solution)/shard_map/scatter | solution.py:77
  80.9 1.4 copy.231
  82.4 3.6 %all-to-all-start.2 = ((bf16[8,4,256,128]{3,2,0,1:T(8,128)(2,1)}), bf16[8,4,256,128]{3,2,0,1:T(8,128)(2,1)S(1)}, u32[]{:S(2)}, u32[]{:S(2)}) async-start(bf16[8,4,256,128]{3,2,0,1:T(8,128)(2,1)} %copy.231), calls=%async_computation.2 | async-start | bytes 4194304 | tf_op jit(solution)/shard_map/all_to_all | solution.py:88
  86.0 0.6 copy.226
  86.6 41.4 %all-to-all-done.2 = bf16[8,4,256,128]{3,2,0,1:T(8,128)(2,1)S(1)} async-done(((bf16[8,4,256,128]{3,2,0,1:T(8,128)(2,1)}), bf16[8,4,256,128]{3,2,0,1:T(8,128)(2,1)S(1)}, u32[]{:S(2)}, u32[]{:S(2)}) %all-to-all-start.2) | async-done | bytes 2097184 | tf_op jit(solution)/shard_map/all_to_all | solution.py:88
  128.0 5.5 %all-to-all-start.1 = ((s32[8,4,256]{2,1,0:T(4,128)}), s32[8,4,256]{2,1,0:T(4,128)S(1)}, u32[]{:S(2)}, u32[]{:S(2)}) async-start(s32[8,4,256]{2,1,0:T(4,128)} %copy.226), calls=%async_computation.1 | async-start | bytes 65536 | tf_op jit(solution)/shard_map/all_to_all | solution.py:94
  133.5 1.4 copy.232
  135.0 5.2 %all-to-all-done.1 = s32[8,4,256]{2,1,0:T(4,128)S(1)} async-done(((s32[8,4,256]{2,1,0:T(4,128)}), s32[8,4,256]{2,1,0:T(4,128)S(1)}, u32[]{:S(2)}, u32[]{:S(2)}) %all-to-all-start.1) | async-done | bytes 32800 | tf_op jit(solution)/shard_map/all_to_all | solution.py:94
  140.2 3.8 %all-to-all-start.3 = ((bf16[8,4,256,128]{3,2,1,0:T(8,128)(2,1)}), bf16[8,4,256,128]{3,2,1,0:T(8,128)(2,1)S(1)}, u32[]{:S(2)}, u32[]{:S(2)}) async-start(bf16[8,4,256,128]{3,2,1,0:T(8,128)(2,1)} %copy.232), calls=%async_computation.3 | async-start | bytes 4194304 | tf_op jit(solution)/shard_map/all_to_all | solution.py:87
  144.0 47.3 %all-to-all-done.3 = bf16[8,4,256,128]{3,2,1,0:T(8,128)(2,1)S(1)} async-done(((bf16[8,4,256,128]{3,2,1,0:T(8,128)(2,1)}), bf16[8,4,256,128]{3,2,1,0:T(8,128)(2,1)S(1)}, u32[]{:S(2)}, u32[]{:S(2)}) %all-to-all-start.3) | async-done | bytes 2097184 | tf_op jit(solution)/shard_map/all_to_all | solution.py:87
  191.4 55.8 %scatter_custom_fusion.2 = f32[2049,128]{1,0:T(8,128)S(1)} fusion(s32[8192]{0:T(1024)S(1)} %bitcast.65, bf16[8192,128]{1,0:T(8,128)(2,1)S(1)} %bitcast.58, f32[]{:T(128)} %constant.21.clone.1), kind=kCustom, calls=%fused_computation.4 | custom fusion | flops 2097152 | bytes 3146244 | tf_op jit(solution)/shard_map/scatter-add | solution.py:102
  247.2 1.0 slice_bitcast_fusion
  248.2 6.8 %reduce_sum.27 = f32[7,128,128]{2,1,0:T(8,128)} reduce(f32[32,7,128,128]{3,2,1,0:T(8,128)} %bitcast.57, f32[]{:T(128)} %constant.21.clone.1), dimensions={0}, to_apply=%region_0.0 | reduce | flops 3555328 | bytes 15138820 | tf_op jit(solution)/shard_map/reduce_sum | solution.py:36
  (162 shorter events, 2.2 us)
Async XLA Ops:
  7.2 10.3 %copy-start = (s32[8,8192]{1,0:T(8,128)S(1)}, s32[8,8192]{1,0:T(8,128)}, u32[]{:S(2)}) copy-start(s32[8,8192]{1,0:T(8,128)} %param.11) | copy-start | bytes 786436
  7.2 2.1 copy-start.1
  7.2 241.0 %all-gather.3.cloned.1.call-start = ((), (), s32[]{:S(2)}) async-start(), calls=%async_computation.4 | async-start | bytes 15138816 | tf_op jit(solution)/shard_map/all_gather | solution.py:36
  10.3 5.4 %copy-start.48 = (bf16[128,1,128]{0,2,1:T(8,128)(2,1)}, bf16[128,1,128]{0,2,1:T(8,128)(2,1)S(1)}, u32[]{:S(2)}) copy-start(bf16[128,1,128]{0,2,1:T(8,128)(2,1)S(1)} %copy.238) | copy-start | bytes 98308
  10.5 5.2 %copy-start.38 = (bf16[128,1,128]{0,2,1:T(8,128)(2,1)}, bf16[128,1,128]{0,2,1:T(8,128)(2,1)S(1)}, u32[]{:S(2)}) copy-start(bf16[128,1,128]{0,2,1:T(8,128)(2,1)S(1)} %copy.240) | copy-start | bytes 98308
  10.6 5.1 %copy-start.36 = (bf16[128,1,128]{0,2,1:T(8,128)(2,1)}, bf16[128,1,128]{0,2,1:T(8,128)(2,1)S(1)}, u32[]{:S(2)}) copy-start(bf16[128,1,128]{0,2,1:T(8,128)(2,1)S(1)} %copy.242) | copy-start | bytes 98308
  10.7 5.0 %copy-start.60 = (bf16[128,1,128]{0,2,1:T(8,128)(2,1)}, bf16[128,1,128]{0,2,1:T(8,128)(2,1)S(1)}, u32[]{:S(2)}) copy-start(bf16[128,1,128]{0,2,1:T(8,128)(2,1)S(1)} %copy.244) | copy-start | bytes 98308
  10.9 4.9 %copy-start.34 = (bf16[128,1,128]{0,2,1:T(8,128)(2,1)}, bf16[128,1,128]{0,2,1:T(8,128)(2,1)S(1)}, u32[]{:S(2)}) copy-start(bf16[128,1,128]{0,2,1:T(8,128)(2,1)S(1)} %copy.246) | copy-start | bytes 98308
  11.0 4.8 %copy-start.58 = (bf16[128,1,128]{0,2,1:T(8,128)(2,1)}, bf16[128,1,128]{0,2,1:T(8,128)(2,1)S(1)}, u32[]{:S(2)}) copy-start(bf16[128,1,128]{0,2,1:T(8,128)(2,1)S(1)} %copy.248) | copy-start | bytes 98308
  11.1 4.6 %copy-start.32 = (bf16[128,1,128]{0,2,1:T(8,128)(2,1)}, bf16[128,1,128]{0,2,1:T(8,128)(2,1)S(1)}, u32[]{:S(2)}) copy-start(bf16[128,1,128]{0,2,1:T(8,128)(2,1)S(1)} %copy.250) | copy-start | bytes 98308
  11.6 4.1 %copy-start.52 = (bf16[128,1,128]{0,2,1:T(8,128)(2,1)}, bf16[128,1,128]{0,2,1:T(8,128)(2,1)S(1)}, u32[]{:S(2)}) copy-start(bf16[128,1,128]{0,2,1:T(8,128)(2,1)S(1)} %copy.254) | copy-start | bytes 98308
  11.8 2.8 %copy-start.20 = (bf16[128,1,128]{0,2,1:T(8,128)(2,1)}, bf16[128,1,128]{0,2,1:T(8,128)(2,1)S(1)}, u32[]{:S(2)}) copy-start(bf16[128,1,128]{0,2,1:T(8,128)(2,1)S(1)} %copy.255) | copy-start | bytes 98308
  11.9 3.9 %copy-start.50 = (bf16[128,1,128]{0,2,1:T(8,128)(2,1)}, bf16[128,1,128]{0,2,1:T(8,128)(2,1)S(1)}, u32[]{:S(2)}) copy-start(bf16[128,1,128]{0,2,1:T(8,128)(2,1)S(1)} %copy.256) | copy-start | bytes 98308
  12.0 2.6 copy-start.18
  12.1 4.6 %copy-start.28 = (bf16[128,1,128]{0,2,1:T(8,128)(2,1)}, bf16[128,1,128]{0,2,1:T(8,128)(2,1)S(1)}, u32[]{:S(2)}) copy-start(bf16[128,1,128]{0,2,1:T(8,128)(2,1)S(1)} %copy.252) | copy-start | bytes 98308
  12.3 4.5 %copy-start.26 = (bf16[128,1,128]{0,2,1:T(8,128)(2,1)}, bf16[128,1,128]{0,2,1:T(8,128)(2,1)S(1)}, u32[]{:S(2)}) copy-start(bf16[128,1,128]{0,2,1:T(8,128)(2,1)S(1)} %copy.253) | copy-start | bytes 98308
  12.4 4.4 %copy-start.30 = (bf16[128,1,128]{0,2,1:T(8,128)(2,1)}, bf16[128,1,128]{0,2,1:T(8,128)(2,1)S(1)}, u32[]{:S(2)}) copy-start(bf16[128,1,128]{0,2,1:T(8,128)(2,1)S(1)} %copy.258) | copy-start | bytes 98308
  12.5 4.2 %copy-start.56 = (bf16[128,1,128]{0,2,1:T(8,128)(2,1)}, bf16[128,1,128]{0,2,1:T(8,128)(2,1)S(1)}, u32[]{:S(2)}) copy-start(bf16[128,1,128]{0,2,1:T(8,128)(2,1)S(1)} %copy.259) | copy-start | bytes 98308
  12.6 4.1 %copy-start.24 = (bf16[128,1,128]{0,2,1:T(8,128)(2,1)}, bf16[128,1,128]{0,2,1:T(8,128)(2,1)S(1)}, u32[]{:S(2)}) copy-start(bf16[128,1,128]{0,2,1:T(8,128)(2,1)S(1)} %copy.260) | copy-start | bytes 98308
  12.8 4.0 %copy-start.54 = (bf16[128,1,128]{0,2,1:T(8,128)(2,1)}, bf16[128,1,128]{0,2,1:T(8,128)(2,1)S(1)}, u32[]{:S(2)}) copy-start(bf16[128,1,128]{0,2,1:T(8,128)(2,1)S(1)} %copy.261) | copy-start | bytes 98308
  12.9 1.7 copy-start.22
  13.0 3.8 %copy-start.46 = (bf16[128,1,128]{0,2,1:T(8,128)(2,1)}, bf16[128,1,128]{0,2,1:T(8,128)(2,1)S(1)}, u32[]{:S(2)}) copy-start(bf16[128,1,128]{0,2,1:T(8,128)(2,1)S(1)} %copy.263) | copy-start | bytes 98308
  13.2 1.5 copy-start.14
  13.3 3.5 %copy-start.40 = (bf16[128,1,128]{0,2,1:T(8,128)(2,1)}, bf16[128,1,128]{0,2,1:T(8,128)(2,1)S(1)}, u32[]{:S(2)}) copy-start(bf16[128,1,128]{0,2,1:T(8,128)(2,1)S(1)} %copy.265) | copy-start | bytes 98308
  13.4 1.2 copy-start.6
  13.7 3.2 %copy-start.42 = (bf16[128,1,128]{0,2,1:T(8,128)(2,1)}, bf16[128,1,128]{0,2,1:T(8,128)(2,1)S(1)}, u32[]{:S(2)}) copy-start(bf16[128,1,128]{0,2,1:T(8,128)(2,1)S(1)} %copy.268) | copy-start | bytes 98308
  13.9 2.9 %copy-start.44 = (bf16[128,1,128]{0,2,1:T(8,128)(2,1)}, bf16[128,1,128]{0,2,1:T(8,128)(2,1)S(1)}, u32[]{:S(2)}) copy-start(bf16[128,1,128]{0,2,1:T(8,128)(2,1)S(1)} %copy.270) | copy-start | bytes 98308
  14.2 2.7 %copy-start.62 = (s32[128,8,4]{0,2,1:T(4,128)S(1)}, s32[128,8,4]{0,2,1:T(4,128)}, u32[]{:S(2)}) copy-start(s32[128,8,4]{0,2,1:T(4,128)} %param.9) | copy-start | bytes 49156
  17.4 26.2 %copy-start.63 = (s32[128,8]{0,1:T(8,128)S(1)}, s32[128,8]{0,1:T(8,128)}, u32[]{:S(2)}) copy-start(s32[128,8]{0,1:T(8,128)} %param.10) | copy-start | bytes 12292
  42.9 22.4 %copy-start.4 = (bf16[128,7,128]{0,2,1:T(8,128)(2,1)S(1)}, bf16[128,7,128]{0,2,1:T(8,128)(2,1)}, u32[]{:S(2)}) copy-start(bf16[128,7,128]{0,2,1:T(8,128)(2,1)} %copy-done.3) | copy-start | bytes 688132
  42.9 22.4 %copy-start.5 = (bf16[7,128,128]{2,1,0:T(8,128)(2,1)S(1)}, bf16[7,128,128]{2,1,0:T(8,128)(2,1)}, u32[]{:S(2)}) copy-start(bf16[7,128,128]{2,1,0:T(8,128)(2,1)} %param.8) | copy-start | bytes 688132
  42.9 22.7 %copy-start.2 = (bf16[128,8,128]{2,1,0:T(8,128)(2,1)S(1)}, bf16[128,8,128]{2,1,0:T(8,128)(2,1)}, u32[]{:S(2)}) copy-start(bf16[128,8,128]{2,1,0:T(8,128)(2,1)} %param.6) | copy-start | bytes 786436
  43.3 22.7 %copy-start.49 = (bf16[128,1,128]{0,2,1:T(8,128)(2,1)S(1)}, bf16[128,1,128]{0,2,1:T(8,128)(2,1)}, u32[]{:S(2)}) copy-start(bf16[128,1,128]{0,2,1:T(8,128)(2,1)} %copy-done.48) | copy-start | bytes 98308
  43.5 22.4 %copy-start.29 = (bf16[128,1,128]{0,2,1:T(8,128)(2,1)S(1)}, bf16[128,1,128]{0,2,1:T(8,128)(2,1)}, u32[]{:S(2)}) copy-start(bf16[128,1,128]{0,2,1:T(8,128)(2,1)} %copy-done.28) | copy-start | bytes 98308
  43.6 22.4 %copy-start.39 = (bf16[128,1,128]{0,2,1:T(8,128)(2,1)S(1)}, bf16[128,1,128]{0,2,1:T(8,128)(2,1)}, u32[]{:S(2)}) copy-start(bf16[128,1,128]{0,2,1:T(8,128)(2,1)} %copy-done.38) | copy-start | bytes 98308
  43.6 22.4 %copy-start.27 = (bf16[128,1,128]{0,2,1:T(8,128)(2,1)S(1)}, bf16[128,1,128]{0,2,1:T(8,128)(2,1)}, u32[]{:S(2)}) copy-start(bf16[128,1,128]{0,2,1:T(8,128)(2,1)} %copy-done.26) | copy-start | bytes 98308
  43.6 22.4 %copy-start.31 = (bf16[128,1,128]{0,2,1:T(8,128)(2,1)S(1)}, bf16[128,1,128]{0,2,1:T(8,128)(2,1)}, u32[]{:S(2)}) copy-start(bf16[128,1,128]{0,2,1:T(8,128)(2,1)} %copy-done.30) | copy-start | bytes 98308
  43.6 22.4 %copy-start.37 = (bf16[128,1,128]{0,2,1:T(8,128)(2,1)S(1)}, bf16[128,1,128]{0,2,1:T(8,128)(2,1)}, u32[]{:S(2)}) copy-start(bf16[128,1,128]{0,2,1:T(8,128)(2,1)} %copy-done.36) | copy-start | bytes 98308
  44.3 21.8 %copy-start.47 = (bf16[128,1,128]{0,2,1:T(8,128)(2,1)S(1)}, bf16[128,1,128]{0,2,1:T(8,128)(2,1)}, u32[]{:S(2)}) copy-start(bf16[128,1,128]{0,2,1:T(8,128)(2,1)} %copy-done.46) | copy-start | bytes 98308
  44.3 21.8 %copy-start.53 = (bf16[128,1,128]{0,2,1:T(8,128)(2,1)S(1)}, bf16[128,1,128]{0,2,1:T(8,128)(2,1)}, u32[]{:S(2)}) copy-start(bf16[128,1,128]{0,2,1:T(8,128)(2,1)} %copy-done.52) | copy-start | bytes 98308
  44.3 21.8 %copy-start.57 = (bf16[128,1,128]{0,2,1:T(8,128)(2,1)S(1)}, bf16[128,1,128]{0,2,1:T(8,128)(2,1)}, u32[]{:S(2)}) copy-start(bf16[128,1,128]{0,2,1:T(8,128)(2,1)} %copy-done.56) | copy-start | bytes 98308
  44.3 21.8 %copy-start.61 = (bf16[128,1,128]{0,2,1:T(8,128)(2,1)S(1)}, bf16[128,1,128]{0,2,1:T(8,128)(2,1)}, u32[]{:S(2)}) copy-start(bf16[128,1,128]{0,2,1:T(8,128)(2,1)} %copy-done.60) | copy-start | bytes 98308
  44.3 21.8 %copy-start.15 = (bf16[128,1,128]{0,2,1:T(8,128)(2,1)S(1)}, bf16[128,1,128]{0,2,1:T(8,128)(2,1)}, u32[]{:S(2)}) copy-start(bf16[128,1,128]{0,2,1:T(8,128)(2,1)} %copy-done.14) | copy-start | bytes 98308
  44.4 21.8 %copy-start.17 = (bf16[128,1,128]{0,2,1:T(8,128)(2,1)S(1)}, bf16[128,1,128]{0,2,1:T(8,128)(2,1)}, u32[]{:S(2)}) copy-start(bf16[128,1,128]{0,2,1:T(8,128)(2,1)} %copy-done.16) | copy-start | bytes 98308
  44.4 21.8 %copy-start.21 = (bf16[128,1,128]{0,2,1:T(8,128)(2,1)S(1)}, bf16[128,1,128]{0,2,1:T(8,128)(2,1)}, u32[]{:S(2)}) copy-start(bf16[128,1,128]{0,2,1:T(8,128)(2,1)} %copy-done.20) | copy-start | bytes 98308
  44.4 21.8 %copy-start.25 = (bf16[128,1,128]{0,2,1:T(8,128)(2,1)S(1)}, bf16[128,1,128]{0,2,1:T(8,128)(2,1)}, u32[]{:S(2)}) copy-start(bf16[128,1,128]{0,2,1:T(8,128)(2,1)} %copy-done.24) | copy-start | bytes 98308
  44.4 21.8 %copy-start.35 = (bf16[128,1,128]{0,2,1:T(8,128)(2,1)S(1)}, bf16[128,1,128]{0,2,1:T(8,128)(2,1)}, u32[]{:S(2)}) copy-start(bf16[128,1,128]{0,2,1:T(8,128)(2,1)} %copy-done.34) | copy-start | bytes 98308
  44.7 21.6 %copy-start.41 = (bf16[128,1,128]{0,2,1:T(8,128)(2,1)S(1)}, bf16[128,1,128]{0,2,1:T(8,128)(2,1)}, u32[]{:S(2)}) copy-start(bf16[128,1,128]{0,2,1:T(8,128)(2,1)} %copy-done.40) | copy-start | bytes 98308
  44.7 21.6 %copy-start.43 = (bf16[128,1,128]{0,2,1:T(8,128)(2,1)S(1)}, bf16[128,1,128]{0,2,1:T(8,128)(2,1)}, u32[]{:S(2)}) copy-start(bf16[128,1,128]{0,2,1:T(8,128)(2,1)} %copy-done.42) | copy-start | bytes 98308
  44.7 21.6 %copy-start.45 = (bf16[128,1,128]{0,2,1:T(8,128)(2,1)S(1)}, bf16[128,1,128]{0,2,1:T(8,128)(2,1)}, u32[]{:S(2)}) copy-start(bf16[128,1,128]{0,2,1:T(8,128)(2,1)} %copy-done.44) | copy-start | bytes 98308
  44.7 21.6 %copy-start.51 = (bf16[128,1,128]{0,2,1:T(8,128)(2,1)S(1)}, bf16[128,1,128]{0,2,1:T(8,128)(2,1)}, u32[]{:S(2)}) copy-start(bf16[128,1,128]{0,2,1:T(8,128)(2,1)} %copy-done.50) | copy-start | bytes 98308
  44.7 21.6 %copy-start.55 = (bf16[128,1,128]{0,2,1:T(8,128)(2,1)S(1)}, bf16[128,1,128]{0,2,1:T(8,128)(2,1)}, u32[]{:S(2)}) copy-start(bf16[128,1,128]{0,2,1:T(8,128)(2,1)} %copy-done.54) | copy-start | bytes 98308
  44.7 21.6 %copy-start.59 = (bf16[128,1,128]{0,2,1:T(8,128)(2,1)S(1)}, bf16[128,1,128]{0,2,1:T(8,128)(2,1)}, u32[]{:S(2)}) copy-start(bf16[128,1,128]{0,2,1:T(8,128)(2,1)} %copy-done.58) | copy-start | bytes 98308
  61.1 21.3 %all-to-all-start = ((s32[8,4,256]{2,0,1:T(8,128)}), s32[8,4,256]{2,0,1:T(8,128)S(1)}, u32[]{:S(2)}, u32[]{:S(2)}) async-start(s32[8,4,256]{2,0,1:T(8,128)} %copy.225), calls=%async_computation | async-start | bytes 65536 | tf_op jit(solution)/shard_map/all_to_all | solution.py:95
  65.3 1.1 copy-start.7
  65.3 1.1 copy-start.9
  65.3 1.1 copy-start.11
  65.4 1.1 copy-start.13
  65.4 1.1 copy-start.19
  65.4 1.1 copy-start.23
  65.4 1.1 copy-start.33
  82.4 45.7 %all-to-all-start.2 = ((bf16[8,4,256,128]{3,2,0,1:T(8,128)(2,1)}), bf16[8,4,256,128]{3,2,0,1:T(8,128)(2,1)S(1)}, u32[]{:S(2)}, u32[]{:S(2)}) async-start(bf16[8,4,256,128]{3,2,0,1:T(8,128)(2,1)} %copy.231), calls=%async_computation.2 | async-start | bytes 4194304 | tf_op jit(solution)/shard_map/all_to_all | solution.py:88
  128.0 12.2 %all-to-all-start.1 = ((s32[8,4,256]{2,1,0:T(4,128)}), s32[8,4,256]{2,1,0:T(4,128)S(1)}, u32[]{:S(2)}, u32[]{:S(2)}) async-start(s32[8,4,256]{2,1,0:T(4,128)} %copy.226), calls=%async_computation.1 | async-start | bytes 65536 | tf_op jit(solution)/shard_map/all_to_all | solution.py:94
  140.2 51.2 %all-to-all-start.3 = ((bf16[8,4,256,128]{3,2,1,0:T(8,128)(2,1)}), bf16[8,4,256,128]{3,2,1,0:T(8,128)(2,1)S(1)}, u32[]{:S(2)}, u32[]{:S(2)}) async-start(bf16[8,4,256,128]{3,2,1,0:T(8,128)(2,1)} %copy.232), calls=%async_computation.3 | async-start | bytes 4194304 | tf_op jit(solution)/shard_map/all_to_all | solution.py:87
  (5 other events, 3.8 us)
Sparse Core Ops, SparseCore 0:
  17.0 122.2 all-gather.2
